TPU v7x, 32 devices: a whole 2x2x4 slice. The times are simulated.
32 devices in a mesh: group: 2 (over y), ctx: 2 (over x), ep: 8 (over z, core).
Axes of the slice: x: 2, y: 2, z: 4, core: 2. Of those that a mesh axis runs over, the one named last changes fastest.
Arguments:
- q_latent: bfloat16 [512, 16384], P(('group', 'ctx'), 'ep'), parts along dimension 0, may hold values from -48 to 48
- q_rope: bfloat16 [512, 2048], P(('group', 'ctx'), 'ep'), parts along dimension 0, may hold values from -6 to 6
- latent_keys: bfloat16 [1024, 256], P('group', 'ctx'), parts along dimension 0, may hold values from -8 to 8
- rope_keys: bfloat16 [128, 256], P('group', 'ctx'), parts along dimension 0, may hold values from -8 to 8
- w_uv: bfloat16 [32, 512, 128], P('ep'), may hold values from -0.25 to 0.25
- moe_tokens: bfloat16 [4096, 7168], P(('group', 'ep'), 'ctx'), parts along dimension 0, may hold values from -6 to 6
- norm_gain: float32 [7168], P('ctx'), may hold values from 0.1 to 1.9
- expert_ids: int32 [4096, 2], P(('group', 'ep')), parts along dimension 0, may hold values from 0 to 3, all different within a row; in each aligned block of 256 rows (0 to 255, 256 to 511, ...) at most 192 rows name the same one
- route_scale: float32 [4096, 2], P(('group', 'ep')), parts along dimension 0, may hold values from 0.5 to 2.5
- w_gate: bfloat16 [8, 7168, 512], P('ep', 'ctx'), may hold values from -0.0625 to 0.0625
- w_up: bfloat16 [8, 7168, 512], P('ep', 'ctx'), may hold values from -0.0625 to 0.0625
- w_down: bfloat16 [8, 512, 7168], P('ep', None, 'ctx'), may hold values from -0.1875 to 0.1875
Outputs:
- attn_out: bfloat16 [512, 4096], P(('group', 'ctx'), 'ep'), parts along dimension 0
- moe_out: bfloat16 [4096, 7168], P(('group', 'ep'), 'ctx'), parts along dimension 0
There are 2 independent parts, one for each index of `group`. A program takes and returns all parts, laid end to end along the dimension named above; an argument that names none is the same for every part. Nothing has to cross between parts.
Inputs may be any that keep to these rules, and one draw needn't show every extreme that they name: `expert_ids`: each row names 2 different experts; among the rows of one ep index no expert is named more than 192 times, a bound that some block reaches.
All inputs are finite; a program needn't handle non-finite values.
Results may differ from a plain program's by a relative error of at most 0.024.
Values may be sent and summed in bfloat16 or wider, within the bound.
A program may use at most 128 MiB of HBM per device.

v0:
```python
import functools
import jax
import jax.numpy as jnp
from jax import lax
from jax.experimental import pallas as pl
from jax.experimental.pallas import tpu as pltpu
from jax.sharding import PartitionSpec as P

score_scale = 192.0 ** (-0.5)
norm_eps = 1e-06
neg_large = -1e30
PIECES = 2
CHUNKS = 4
SLACK = 1
VMEM_BYTES = 67043328
f32 = jnp.float32
bf16 = jnp.bfloat16


def mm(a, b):
    return jnp.dot(a, b, preferred_element_type=f32)


def mm_t(a, b):
    return lax.dot_general(a, b, (((0,), (0,)), ((), ())), preferred_element_type=f32)


def swap_ctx(x):
    return lax.ppermute(x, "ctx", [(0, 1), (1, 0)])


def gather_keys(mine, ctx):
    if lax.axis_size("ctx") != 2:
        return lax.all_gather(mine, "ctx", axis=1, tiled=True)
    other = swap_ctx(mine)
    first = ctx == 0
    return jnp.concatenate(
        [jnp.where(first, mine, other), jnp.where(first, other, mine)], axis=1
    )


def sum_ctx(x):
    if lax.axis_size("ctx") != 2:
        return lax.psum(x, "ctx")
    return x + swap_ctx(x)


def attention(q_latent, q_rope, latent_keys, rope_keys, w_uv):
    seq_rows = q_latent.shape[0]
    head_count = w_uv.shape[0]
    latent_dim = latent_keys.shape[0]
    rope_dim = rope_keys.shape[0]
    query_lat = (
        q_latent.reshape(seq_rows, head_count, latent_dim)
        .transpose(1, 0, 2)
        .reshape(head_count * seq_rows, latent_dim)
    )
    query_rot = (
        q_rope.reshape(seq_rows, head_count, rope_dim)
        .transpose(1, 0, 2)
        .reshape(head_count * seq_rows, rope_dim)
    )
    ctx = lax.axis_index("ctx")
    query_pos = ctx * seq_rows + jnp.tile(jnp.arange(seq_rows, dtype=jnp.int32), head_count)
    mine = jnp.concatenate([latent_keys, rope_keys], axis=0)
    keys = gather_keys(mine, ctx)
    lat, rope = keys[:latent_dim], keys[latent_dim:]
    scores = (mm(query_lat, lat) + mm(query_rot, rope)) * score_scale
    key_pos = jnp.arange(lat.shape[1], dtype=jnp.int32)
    visible = key_pos[None, :] <= query_pos[:, None]
    masked = jnp.where(visible, scores, neg_large)
    top = jnp.max(masked, axis=1, keepdims=True)
    weights = jnp.where(visible, jnp.exp(masked - top), 0.0)
    total = jnp.sum(weights, axis=1, keepdims=True)
    update = lax.dot_general(
        weights.astype(bf16), lat, (((1,), (1,)), ((), ())), preferred_element_type=f32
    )
    context = (update / total).astype(bf16).reshape(head_count, seq_rows, latent_dim)
    heads = jnp.einsum("hsl,hlv->shv", context, w_uv, preferred_element_type=f32)
    return heads.reshape(seq_rows, head_count * w_uv.shape[2]).astype(bf16)


def ranks(key):
    n = key.shape[0]
    at = jnp.arange(n, dtype=jnp.int32)
    ahead = (key[None, :] > key[:, None]) | (
        (key[None, :] == key[:, None]) & (at[None, :] < at[:, None])
    )
    return jnp.sum(ahead.astype(jnp.int32), axis=1)


def position(ids, to_right):
    return ranks(jnp.where(to_right, jnp.max(ids, axis=1), -jnp.min(ids, axis=1)))


def hop_body(
    q_latent,
    q_rope,
    latent_keys,
    rope_keys,
    w_uv,
    moe_tokens,
    norm_gain,
    expert_ids,
    route_scale,
    w_gate,
    w_up,
    w_down,
):
    n_ep = lax.axis_size("ep")
    nz = n_ep // 2
    rows, top_count = expert_ids.shape
    cap = min(rows, 3 * rows * top_count // (2 * nz))
    half = cap // 2
    width = moe_tokens.shape[1]
    ep = lax.axis_index("ep")
    z = ep // 2
    ctx = lax.axis_index("ctx")
    group = -(-128 // cap)
    bands = [
        (b, cap * b, min(rows, cap * (b + group)))
        for b in range(0, nz - 1, group)
        if cap * b < rows
    ]
    pieces = max(1, PIECES * width // 3584)

    def hop(x, pairs):
        return lax.ppermute(
            x, "ep", [(2 * a + c, 2 * b + c) for a, b in pairs for c in range(2)]
        )

    info = jnp.concatenate([expert_ids.astype(f32), route_scale], axis=1)
    infos = {0: info}
    for k in range(1, nz):
        infos[k] = hop(info, [(a, (a + k) % nz) for a in range(nz)])

    def partner(x):
        return lax.ppermute(x, "ep", [(i, i ^ 1) for i in range(n_ep)])

    wide = moe_tokens.astype(f32)
    local_sq = jnp.sum(wide * wide, axis=1)
    total_sq = sum_ctx(local_sq)
    scale_rows = lax.rsqrt(total_sq / (width * lax.axis_size("ctx")) + norm_eps)
    normed = (wide * scale_rows[:, None] * norm_gain[None, :]).astype(bf16)

    slots = jnp.arange(rows, dtype=jnp.int32)
    pos_right = position(expert_ids, True)
    pos_left = position(expert_ids, False)
    perm_right = (pos_right[None, :] == slots[:, None]).astype(bf16)
    perm_left = (pos_left[None, :] == slots[:, None]).astype(bf16)

    gates = [w_gate[0], partner(w_gate[0])]
    ups = [w_up[0], partner(w_up[0])]
    downs = [w_down[0], partner(w_down[0])]

    held = {}
    for to_right, perm in ((True, perm_right), (False, perm_left)):
        for b, lo, hi in bands:
            block = mm(perm[lo:hi], normed).astype(bf16)
            for k in range(1, nz):
                if to_right:
                    pairs = [(a, a + 1) for a in range(k - 1, nz - 1 - b)]
                else:
                    pairs = [(nz - 1 - a, nz - 2 - a) for a in range(k - 1, nz - 1 - b)]
                if not pairs:
                    break
                block = hop(block, pairs)
                held[to_right, k, b] = block

    def chunk_of(zz, j):
        m = min(zz, nz - 1 - zz)
        if j <= 2 * m:
            return (j % 2 == 1, (j + 1) // 2)
        return (zz > nz - 1 - zz, j - m)

    expert = z

    def picks(ids, scales):
        hits = jnp.any(ids == expert, axis=1)
        at = jnp.arange(rows, dtype=jnp.int32)
        before = hits[None, :] & (at[None, :] < at[:, None])
        slot = jnp.sum(before.astype(jnp.int32), axis=1)
        sel = hits[None, :] & (slot[None, :] == jnp.arange(cap, dtype=jnp.int32)[:, None])
        own = jnp.sum(jnp.where(ids == expert, scales, 0.0), axis=1)
        return sel.astype(bf16), own

    def hidden_of(rows_in, sel):
        parts = jnp.concatenate(
            [mm(rows_in, w) for w in (gates[0], gates[1], ups[0], ups[1])], axis=1
        )
        units = parts.shape[1] // 2

        def act(both):
            return (jax.nn.silu(both[:, :units]) * both[:, units:]).astype(bf16)

        if lax.axis_size("ctx") != 2:
            both = lax.psum_scatter(parts.astype(bf16), "ctx", scatter_dimension=0, tiled=True)
            hid = lax.all_gather(act(both.astype(f32)), "ctx", axis=0, tiled=True)
            return mm_t(sel, hid).astype(bf16)
        theirs = lax.dynamic_slice_in_dim(parts, (1 - ctx) * half, half, 0).astype(bf16)
        mine = lax.dynamic_slice_in_dim(parts, ctx * half, half, 0)
        hid = act(mine + swap_ctx(theirs).astype(f32))
        hid_other = swap_ctx(hid)
        sel_mine = lax.dynamic_slice_in_dim(sel, ctx * half, half, 0)
        sel_other = lax.dynamic_slice_in_dim(sel, (1 - ctx) * half, half, 0)
        return (mm_t(sel_mine, hid) + mm_t(sel_other, hid_other)).astype(bf16)

    fh = w_gate.shape[2]
    step = width // pieces

    def contribution(hid, scale, piece):
        cols = slice(piece * step, (piece + 1) * step)
        out = mm(hid[:, :fh], downs[0][:, cols]) + mm(hid[:, fh:], downs[1][:, cols])
        return out * scale[:, None]

    sel_own, scale_own = picks(expert_ids, route_scale)
    hid_own = hidden_of(mm(sel_own, normed).astype(bf16), sel_own)

    hids = {}
    for j in range(1, nz):
        kinds = [chunk_of(zz, j) for zz in range(nz)]
        distinct = sorted(set(kinds))

        def choose(get):
            value = None
            for kind in distinct:
                here = False
                for zz in range(nz):
                    if kinds[zz] == kind:
                        here = here | (z == zz)
                got = get(kind)
                if got is None:
                    continue
                value = got if value is None else jnp.where(here, got, value)
            return value

        def source_info(kind):
            to_right, k = kind
            return infos[k] if to_right else infos[nz - k]

        chosen = choose(source_info)
        from_left = choose(lambda kind: jnp.full((1,), kind[0], jnp.bool_))[0]
        ids = chosen[:, :top_count].astype(jnp.int32)
        sel, scale = picks(ids, chosen[:, top_count:])
        pos = position(ids, from_left)
        place = (pos[:, None] == slots[None, :]).astype(bf16)
        sel_at = mm(sel, place).astype(bf16)
        scale_at = jnp.sum(jnp.where(pos[:, None] == slots[None, :], scale[:, None], 0.0), axis=0)
        rows_in = None
        for b, lo, hi in bands:
            block = choose(lambda kind: held.get((kind[0], kind[1], b)))
            if block is None:
                continue
            part = mm(sel_at[:, lo:hi], block)
            rows_in = part if rows_in is None else rows_in + part
        hids[j] = (hidden_of(rows_in.astype(bf16), sel_at), scale_at, kinds)

    def chunk_for(to_right, k):
        hid = scale = None
        for j in range(1, nz):
            zs = [zz for zz in range(nz) if hids[j][2][zz] == (to_right, k)]
            if not zs:
                continue
            here = False
            for zz in zs:
                here = here | (z == zz)
            if hid is None:
                hid = jnp.where(here, hids[j][0], 0)
                scale = jnp.where(here, hids[j][1], 0)
            else:
                hid = jnp.where(here, hids[j][0], hid)
                scale = jnp.where(here, hids[j][1], scale)
        return hid, scale

    returned = {}
    for k in range(nz - 1, 0, -1):
        for to_right in (True, False):
            hid, scale = chunk_for(to_right, k)
            for piece in range(pieces):
                acc = contribution(hid, scale, piece)
                for b, lo, hi in bands:
                    value = acc[lo:hi]
                    before = returned.get((to_right, piece, b))
                    if before is not None:
                        value = value + before.astype(f32)
                    pairs = [(a + 1, a) for a in range(k - 1, nz - 1 - b)]
                    if not to_right:
                        pairs = [(nz - 1 - p, nz - 1 - q) for p, q in pairs]
                    if pairs:
                        returned[to_right, piece, b] = hop(value.astype(bf16), pairs)

    outs = []
    for piece in range(pieces):
        acc = contribution(hid_own, scale_own, piece)
        for to_right, perm in ((True, perm_right), (False, perm_left)):
            for b, lo, hi in bands:
                got = returned.get((to_right, piece, b))
                if got is not None:
                    acc = acc + mm_t(perm[lo:hi], got)
        outs.append(acc.astype(bf16))
    moe_out = jnp.concatenate(outs, axis=1)
    attn_out = attention(q_latent, q_rope, latent_keys, rope_keys, w_uv)
    return (attn_out, moe_out)


def expert_kernel(
    nz,
    chunks,
    total_width,
    x_hbm,
    wg_hbm,
    wu_hbm,
    wd_hbm,
    gain_ref,
    route_ref,
    out_hbm,
    xs,
    wgu,
    wd,
    ret,
    con,
    theirs,
    mine,
    outgoing,
    scaled,
    squares,
    squares_in,
    routes,
    local_sem,
    w_send,
    w_recv,
    x_send,
    x_recv,
    r_send,
    r_recv,
    p_send,
    p_recv,
    q_send,
    q_recv,
    t_send,
    t_recv,
    o_sem,
):
    ep = lax.axis_index("ep")
    z = ep // 2
    core = ep % 2
    ctx = lax.axis_index("ctx")
    rows, width = xs.shape[1], xs.shape[2]
    fh = wgu.shape[2]
    groups = rows // 8
    last = nz - 1
    spans = last * chunks
    left, right = {"ep": ep - 2}, {"ep": ep + 2}
    across = {"ctx": 1 - ctx}
    beside = {"ep": 2 * z + 1 - core}

    def remote(src, dst, send, recv, device):
        return pltpu.make_async_remote_copy(
            src_ref=src,
            dst_ref=dst,
            send_sem=send,
            recv_sem=recv,
            device_id=device,
            device_id_type=pl.DeviceIdType.MESH,
        )

    barrier = pltpu.get_barrier_semaphore()
    for step in range(1, nz):
        pl.semaphore_signal(
            barrier,
            inc=1,
            device_id={"ep": 2 * lax.rem(z + step, nz) + core},
            device_id_type=pl.DeviceIdType.MESH,
        )
    for device in (across, beside):
        pl.semaphore_signal(
            barrier, inc=1, device_id=device, device_id_type=pl.DeviceIdType.MESH
        )

    def own_weights(k):
        if k == 0:
            return pltpu.make_async_copy(wg_hbm.at[0], wgu.at[0], local_sem.at[0])
        if k == 1:
            return pltpu.make_async_copy(wu_hbm.at[0], wgu.at[2], local_sem.at[1])
        return pltpu.make_async_copy(wd_hbm.at[0], wd.at[pl.ds(0, fh), :], local_sem.at[2])

    def give_weights(k):
        src = (wg_hbm, wu_hbm, wd_hbm)[k].at[0]
        dst = (wgu.at[1], wgu.at[3], wd.at[pl.ds(fh, fh), :])[k]
        return remote(src, dst, w_send.at[k], w_recv.at[k], beside)

    def own_rows(i):
        return pltpu.make_async_copy(
            x_hbm.at[pl.ds(i * rows, rows), :], xs.at[z * chunks + i], local_sem.at[3 + i]
        )

    def give_rows(i, to_right):
        side = right if to_right else left
        sem = z * chunks + i if to_right else nz * chunks + i
        return remote(
            x_hbm.at[pl.ds(i * rows, rows), :],
            xs.at[z * chunks + i],
            x_send.at[sem],
            x_recv.at[z * chunks + i],
            side,
        )

    def pass_rows(at, to_right):
        side = right if to_right else left
        return remote(xs.at[at], xs.at[at], x_send.at[at], x_recv.at[at], side)

    def give_routes(step):
        to = lax.rem(z + step, nz)
        return remote(
            route_ref.at[to],
            routes.at[z],
            t_send.at[to],
            t_recv.at[z],
            {"ep": 2 * to + core},
        )

    def await_routes(step):
        of = lax.rem(z + step, nz)
        remote(
            route_ref.at[of], routes.at[of], t_send.at[of], t_recv.at[of], {"ep": 2 * of + core}
        ).wait_recv()

    pl.semaphore_wait(barrier, nz + 1)
    for k in range(2):
        own_weights(k).start()
    for i in range(chunks):

        @pl.when(z < last)
        def _():
            give_rows(i, True).start()

        @pl.when(z > 0)
        def _():
            give_rows(i, False).start()

    for step in range(1, nz):
        give_routes(step).start()
    for k in range(2):
        give_weights(k).start()
    own_weights(2).start()
    give_weights(2).start()
    for i in range(chunks):
        own_rows(i).start()
    routes[z] = route_ref[z]

    row_group = lax.broadcasted_iota(jnp.int32, (rows, 128), 0) // 8
    lane = lax.broadcasted_iota(jnp.int32, (rows, 128), 1)
    block = fh if width % fh == 0 else 128

    def spread(packed, offset):
        tall = jnp.broadcast_to(packed[None], (groups, 8, 128)).reshape(rows, 128)
        return jnp.sum(jnp.where(lane == row_group + offset, tall, 0.0), axis=1, keepdims=True)

    def exchange(at, slot):
        return (
            remote(outgoing.at[slot], theirs.at[at], p_send.at[at], p_recv.at[at], across),
            remote(squares.at[slot], squares_in.at[at], q_send.at[at], q_recv.at[at], across),
        )

    def project(at, slot):
        def normalise(n, total):
            cols = pl.ds(pl.multiple_of(n * block, block), block)
            wide = xs[at, :, cols].astype(f32)
            scaled[:, cols] = (wide * gain_ref[:, cols]).astype(bf16)
            square = wide * wide
            for m in range(block // 128):
                total = total + square[:, m * 128 : (m + 1) * 128]
            return total

        total = lax.fori_loop(0, width // block, normalise, jnp.zeros((rows, 128), f32))
        column = jnp.sum(total, axis=1, keepdims=True)
        packed = jnp.where(lane == row_group, jnp.broadcast_to(column, (rows, 128)), 0.0)
        squares[slot] = jnp.sum(packed.reshape(groups, 8, 128), axis=0)

        @pl.loop(0, 4)
        def _(k):
            part = jnp.dot(scaled[...], wgu[k], preferred_element_type=f32)
            mine[slot, k] = part
            outgoing[slot, k] = part.astype(bf16)

        for copy in exchange(at, slot):
            copy.start()

    def expand(source, i, at, slot):
        for copy in exchange(at, slot):
            copy.wait()
        scale = lax.rsqrt(spread(squares[slot] + squares_in[at], 0) / total_width + norm_eps)
        weight = spread(routes[source], i * groups)

        @pl.loop(0, 2)
        def _(b):
            gate = (mine[slot, b] + theirs[at, b].astype(f32)) * scale
            up = (mine[slot, b + 2] + theirs[at, b + 2].astype(f32)) * scale
            hid = jax.nn.silu(gate) * up * weight
            scaled[:, pl.ds(pl.multiple_of(b * fh, fh), fh)] = hid.astype(bf16)

        @pl.loop(0, width // block)
        def _(n):
            cols = pl.ds(pl.multiple_of(n * block, block), block)
            con[at, :, cols] = jnp.dot(
                scaled[:, : 2 * fh], wd[:, cols], preferred_element_type=f32
            ).astype(bf16)

    def place(t, q):
        hop, i = t // chunks, lax.rem(t, chunks)
        source = jnp.where(q == 0, z - 1 - hop, jnp.where(q == 1, z + 1 + hop, z))
        there = (t >= 0) & (t < spans) & (source >= 0) & (source <= last)
        there = there & ((q < 2) | (hop == last - 1))
        return source, i, there

    def give_back(source, i, to_left):
        at = source * chunks + i
        to = at if to_left else at + chunks
        side = left if to_left else right
        return remote(con.at[at], ret.at[to], r_send.at[at], r_recv.at[to], side)

    def await_back(source, i, to_left):
        at = source * chunks + i
        to = at if to_left else at + chunks
        remote(con.at[at], ret.at[to], r_send.at[at], r_recv.at[to], left).wait_recv()
        return to

    def add_back(source, i, tos):
        at = source * chunks + i

        @pl.loop(0, width // block)
        def _(n):
            cols = pl.ds(pl.multiple_of(n * block, block), block)
            value = con[at, :, cols].astype(f32)
            for to in tos:
                value = value + ret[to, :, cols].astype(f32)
            con[at, :, cols] = value.astype(bf16)

    def event(k, near):
        kept = jnp.maximum(near - 1 - SLACK, 0)
        first = chunks - kept
        rest = k - first
        is_first = k < first
        is_mid = rest < (near - 1) * chunks
        hop = jnp.where(is_first, 0, jnp.where(is_mid, 1 + rest // chunks, 0))
        i = jnp.where(
            is_first, k, jnp.where(is_mid, lax.rem(rest, chunks), first + rest - (near - 1) * chunks)
        )
        return hop, i

    def slot_step(t, carry):
        for q, to_right in ((0, True), (1, False)):
            source, i, there = place(t, q)
            onward = (z < last) if to_right else (z > 0)

            @pl.when(there)
            def _():
                at = source * chunks + i
                pass_rows(at, to_right).wait_recv()

                @pl.when(onward)
                def _():
                    pass_rows(at, to_right).start()

        for to_left in (True, False):
            near = z if to_left else last - z
            k = t + 1 - (nz - near) * chunks
            go = (k >= 0) & (k < near * chunks) & (near < last)

            @pl.when(go)
            def _():
                hop, i = event(k, near)
                source = z - 1 - hop if to_left else z + 1 + hop
                to = await_back(source, i, to_left)
                add_back(source, i, [to])
                give_back(source, i, to_left).start()

        @pl.when(t == 0)
        def _():
            for k in range(2):
                own_weights(k).wait()
                give_weights(k).wait()

        @pl.loop(0, 3)
        def _(q):
            source, i, there = place(t, q)

            @pl.when(there)
            def _():
                project(source * chunks + i, lax.rem(t, 2) * 3 + q)

        @pl.when(t == 1)
        def _():
            own_weights(2).wait()
            give_weights(2).wait()
            for step in range(1, nz):
                await_routes(step)

        @pl.loop(0, 3)
        def _(q):
            source, i, there = place(t - 1, q)

            @pl.when(there)
            def _():
                expand(source, i, source * chunks + i, lax.rem(t + 1, 2) * 3 + q)

        for to_left in (True, False):
            near = z if to_left else last - z
            source, i, there = place(t - 1, 0 if to_left else 1)
            kept = jnp.maximum(near - 1 - SLACK, 0)
            held = (t - 1 < chunks) & (i >= chunks - kept)

            @pl.when(there & (near == last) & jnp.logical_not(held))
            def _():
                give_back(source, i, to_left).start()

            @pl.when((near == last) & (t == spans + 1))
            def _():
                for n in range(chunks):

                    @pl.when(n >= chunks - kept)
                    def _():
                        give_back(z - 1 if to_left else z + 1, n, to_left).start()

        return carry

    for i in range(chunks):
        own_rows(i).wait()
    lax.fori_loop(0, nz * chunks, slot_step, 0)

    def finish(i):
        at = z * chunks + i

        @pl.when(z < last)
        def _():
            to = await_back(z, i, True)
            add_back(z, i, [to])

        @pl.when(z > 0)
        def _():
            to = await_back(z, i, False)
            add_back(z, i, [to])

        return pltpu.make_async_copy(
            con.at[at], out_hbm.at[pl.ds(i * rows, rows), :], o_sem.at[i]
        )

    for i in range(chunks):
        finish(i).start()

    for i in range(chunks):
        at = z * chunks + i
        pltpu.make_async_copy(
            con.at[at], out_hbm.at[pl.ds(i * rows, rows), :], o_sem.at[i]
        ).wait()

        @pl.when(z < last)
        def _():
            give_rows(i, True).wait_send()

        @pl.when(z > 0)
        def _():
            give_rows(i, False).wait_send()

    for step in range(1, nz):
        give_routes(step).wait_send()

    def settle(t, carry):
        for q, to_right in ((0, True), (1, False)):
            source, i, there = place(t, q)
            onward = (z < last) if to_right else (z > 0)

            @pl.when(there)
            def _():
                give_back(source, i, to_right).wait_send()

                @pl.when(onward)
                def _():
                    pass_rows(source * chunks + i, to_right).wait_send()

        return carry

    lax.fori_loop(0, spans, settle, 0)


def expert_scratch(nz, rows, width, fh):
    jobs = nz * CHUNKS
    dma = pltpu.SemaphoreType.DMA
    return [
        pltpu.VMEM((jobs, rows, width), bf16),
        pltpu.VMEM((4, width, fh), bf16),
        pltpu.VMEM((2 * fh, width), bf16),
        pltpu.VMEM((jobs + CHUNKS, rows, width), bf16),
        pltpu.VMEM((jobs, rows, width), bf16),
        pltpu.VMEM((jobs, 4, rows, fh), bf16),
        pltpu.VMEM((6, 4, rows, fh), f32),
        pltpu.VMEM((6, 4, rows, fh), bf16),
        pltpu.VMEM((rows, width), bf16),
        pltpu.VMEM((6, 8, 128), f32),
        pltpu.VMEM((jobs, 8, 128), f32),
        pltpu.VMEM((nz, 8, 128), f32),
        dma((3 + CHUNKS,)),
        dma((3,)),
        dma((3,)),
        dma((jobs + CHUNKS,)),
        dma((jobs,)),
        dma((jobs,)),
        dma((jobs + CHUNKS,)),
        dma((jobs,)),
        dma((jobs,)),
        dma((jobs,)),
        dma((jobs,)),
        dma((nz,)),
        dma((nz,)),
        dma((CHUNKS,)),
    ]


def scratch_bytes(shapes):
    total = 0
    for s in shapes:
        if s.memory_space == pltpu.VMEM:
            n = jnp.dtype(s.dtype).itemsize
            for d in s.shape:
                n *= d
            total += n
    return total


def fits(moe_tokens, w_gate):
    n_ep = lax.axis_size("ep")
    nz = n_ep // 2
    tokens, width = moe_tokens.shape
    fh = w_gate.shape[2]
    rows = tokens // CHUNKS
    if lax.axis_size("ctx") != 2 or n_ep % 2 or nz < 2 or w_gate.shape[0] != 1:
        return False
    if tokens % (16 * CHUNKS) or tokens > 1024 or width % 128 or fh % 128:
        return False
    return scratch_bytes(expert_scratch(nz, rows, width, fh)) < VMEM_BYTES - 2**21


def experts(moe_tokens, norm_gain, expert_ids, route_scale, w_gate, w_up, w_down):
    nz = lax.axis_size("ep") // 2
    tokens, width = moe_tokens.shape
    fh = w_gate.shape[2]
    rows = tokens // CHUNKS
    named = expert_ids[None] == jnp.arange(nz, dtype=jnp.int32)[:, None, None]
    table = jnp.sum(jnp.where(named, route_scale[None], 0.0), axis=2)
    table = table.reshape(nz, tokens // 8, 8).transpose(0, 2, 1)
    table = jnp.pad(table, ((0, 0), (0, 0), (0, 128 - tokens // 8)))
    anywhere = pl.BlockSpec(memory_space=pl.ANY)
    whole = pl.BlockSpec(memory_space=pltpu.VMEM)
    return pl.pallas_call(
        functools.partial(expert_kernel, nz, CHUNKS, width * lax.axis_size("ctx")),
        out_shape=jax.ShapeDtypeStruct((tokens, width), bf16),
        in_specs=[anywhere] * 4 + [whole] * 2,
        out_specs=anywhere,
        scratch_shapes=expert_scratch(nz, rows, width, fh),
        compiler_params=pltpu.CompilerParams(
            collective_id=0, has_side_effects=True, vmem_limit_bytes=VMEM_BYTES
        ),
    )(moe_tokens, w_gate, w_up, w_down, norm_gain[None, :], table)


def body(
    q_latent,
    q_rope,
    latent_keys,
    rope_keys,
    w_uv,
    moe_tokens,
    norm_gain,
    expert_ids,
    route_scale,
    w_gate,
    w_up,
    w_down,
):
    if not fits(moe_tokens, w_gate):
        return hop_body(
            q_latent,
            q_rope,
            latent_keys,
            rope_keys,
            w_uv,
            moe_tokens,
            norm_gain,
            expert_ids,
            route_scale,
            w_gate,
            w_up,
            w_down,
        )
    moe_out = experts(moe_tokens, norm_gain, expert_ids, route_scale, w_gate, w_up, w_down)
    attn_out = attention(q_latent, q_rope, latent_keys, rope_keys, w_uv)
    return (attn_out, moe_out)


def solution(mesh):
    return jax.shard_map(
        body,
        mesh=mesh,
        in_specs=(
            P(("group", "ctx"), "ep"),
            P(("group", "ctx"), "ep"),
            P("group", "ctx"),
            P("group", "ctx"),
            P("ep", None, None),
            P(("group", "ep"), "ctx"),
            P("ctx"),
            P(("group", "ep"), None),
            P(("group", "ep"), None),
            P("ep", "ctx", None),
            P("ep", "ctx", None),
            P("ep", None, "ctx"),
        ),
        out_specs=(P(("group", "ctx"), "ep"), P(("group", "ep"), "ctx")),
        check_vma=False,
    )
```

profile of v0, /device:TPU:24, one launch (start us, length us, event | category | flops | bytes accessed | tf_op | source)
XLA Modules:
  0.0 235.0 jit_solution(14131108265139705199)
XLA Ops:
  0.6 1.6 constant_dynamic-update-slice_fusion.1
  2.2 1.3 constant_dynamic-update-slice_fusion
  3.5 1.5 collective-permute-start
  5.0 0.7 select_reduce_fusion
  5.7 1.3 broadcast_in_dim.31.gain_ref
  7.0 0.1 reshape.40
  7.1 0.1 copy.39
  7.2 1.6 copy.36
  8.8 1.3 copy.34
  10.1 1.0 copy.35
  11.1 0.6 pad.4.route_ref
  11.7 216.8 %shard_map.131 = bf16[256,3584]{1,0:T(8,128)(2,1)} custom-call(bf16[256,3584]{1,0:T(8,128)(2,1)} %x_hbm.1, bf16[1,3584,512]{2,1,0:T(8,128)(2,1)} %wg_hbm.1, bf16[1,3584,512]{2,1,0:T(8,128)(2,1)} %wu_hbm.1, bf16[1,512,3584]{2,1,0:T(8,128)(2,1)} %wd_hbm.1, f32[1,3584]{1,0:T(1,128)} %broadcast_in_dim.31.gain_ref, f32[4,8,128]{2,1,0:T(8,128)} %pad.4.route_ref), custom_call_target="tpu_custom_call" | custom-call | tf_op jit(solution)/shard_map/pallas_call | solution.py:754
  228.5 0.0 collective-permute-done
  228.5 1.0 broadcast_select_fusion.1
  229.5 1.1 fusion.11
  230.6 0.0 copy-start.1
  230.6 1.5 fusion.19
  232.1 0.0 copy-start
  232.1 0.1 fusion.4
  232.3 0.4 fusion
  232.6 0.0 copy-done.1
  232.6 0.4 convolution_convert_fusion
  233.0 0.8 copy.40
  233.8 0.0 copy-done
  233.8 1.2 copy.49
  (1 shorter events, 0.0 us)
Async XLA Ops:
  3.5 225.0 %collective-permute-start = (bf16[576,128]{1,0:T(8,128)(2,1)}, bf16[576,128]{1,0:T(8,128)(2,1)}, u32[]{:S(2)}, u32[]{:S(2)}) collective-permute-start(bf16[576,128]{1,0:T(8,128)(2,1)} %constant_dynamic-update-slice_fusion), channel_id=1, source_target_pairs={{0,8},{8,0},{1,9},{9,1},{2,10},{10,2},{3,11},{11,3},{4,12},{12,4},... | collective-permute-start | bytes 442376 | tf_op jit(solution)/shard_map/ppermute | solution.py:29
  230.6 2.0 copy-start.1
  232.1 1.7 copy-start
where the time goes:
time: 236 us; the launch traced here: 235 us
  Pallas kernels  217 us (92%)
  local copies, waits for them, and re-layouts  10.9 us (5%)
  matrix products  3.27 us (1%)
    pallas_call x1, Pallas kernels, experts(): pl.pallas_call(functools.partial(expert_kernel, nz, CHUNKS, width * lax.a...  217 us
    unnamed x9, local copies, waits for them, and re-layouts  6.46 us
  transfers between devices with their start and end apart: 1, of which 0 were waited for; matrix products, arithmetic and copies ran while one was open for 3% of the time, Pallas kernels for 92%

commit v1 on v0

--- a/solution.py
+++ b/solution.py
@@ -11,7 +11,6 @@
 neg_large = -1e30
 PIECES = 2
 CHUNKS = 4
-SLACK = 1
 VMEM_BYTES = 67043328
 f32 = jnp.float32
 bf16 = jnp.bfloat16
@@ -307,13 +306,26 @@
     nz,
     chunks,
     total_width,
+    ql_hbm,
+    qr_hbm,
+    lk_hbm,
+    rk_hbm,
+    uv_hbm,
     x_hbm,
     wg_hbm,
     wu_hbm,
     wd_hbm,
     gain_ref,
-    route_ref,
+    ids_ref,
+    scale_ref,
+    attn_hbm,
     out_hbm,
+    ql,
+    qr,
+    keys,
+    ropes,
+    uv,
+    attn,
     xs,
     wgu,
     wd,
@@ -325,7 +337,11 @@
     scaled,
     squares,
     squares_in,
+    table,
     routes,
+    a_local,
+    a_send,
+    a_recv,
     local_sem,
     w_send,
     w_recv,
@@ -350,6 +366,7 @@
     groups = rows // 8
     last = nz - 1
     spans = last * chunks
+    half = chunks // 2
     left, right = {"ep": ep - 2}, {"ep": ep + 2}
     across = {"ctx": 1 - ctx}
     beside = {"ep": 2 * z + 1 - core}
@@ -412,7 +429,7 @@
     def give_routes(step):
         to = lax.rem(z + step, nz)
         return remote(
-            route_ref.at[to],
+            table.at[to],
             routes.at[z],
             t_send.at[to],
             t_recv.at[z],
@@ -422,13 +439,70 @@
     def await_routes(step):
         of = lax.rem(z + step, nz)
         remote(
-            route_ref.at[of], routes.at[of], t_send.at[of], t_recv.at[of], {"ep": 2 * of + core}
+            table.at[of], routes.at[of], t_send.at[of], t_recv.at[of], {"ep": 2 * of + core}
         ).wait_recv()
 
+    seq = ql.shape[0]
+    latent = keys.shape[0]
+    turn = qr_hbm.shape[1] // uv.shape[0]
+    mine_at = pl.ds(pl.multiple_of(ctx * seq, seq), seq)
+    key_parts = (
+        (lk_hbm, keys.at[:, mine_at]),
+        (rk_hbm, ropes.at[0, pl.ds(0, turn), mine_at]),
+        (rk_hbm, ropes.at[1, pl.ds(turn, turn), mine_at]),
+    )
+
+    def local_attention():
+        pairs = key_parts + ((ql_hbm, ql), (qr_hbm, qr), (uv_hbm, uv))
+        return [
+            pltpu.make_async_copy(src, dst, a_local.at[n]) for n, (src, dst) in enumerate(pairs)
+        ]
+
+    def give_keys():
+        return [
+            remote(src, dst, a_send.at[n], a_recv.at[n], across)
+            for n, (src, dst) in enumerate(key_parts)
+        ]
+
+    def put_attention():
+        return pltpu.make_async_copy(attn, attn_hbm, a_local.at[6])
+
+    def attend(head):
+        span = keys.shape[1]
+        value = uv.shape[2]
+        pair = head // 2
+        query = ctx * seq + lax.broadcasted_iota(jnp.int32, (seq, span), 0)
+        visible = lax.broadcasted_iota(jnp.int32, (seq, span), 1) <= query
+        query_lat = ql[:, pl.ds(pl.multiple_of(head * latent, latent), latent)]
+        query_rot = qr[:, pl.ds(pl.multiple_of(pair * 2 * turn, 2 * turn), 2 * turn)]
+        rotary = ropes[lax.rem(head, 2)]
+        scores = (mm(query_lat, keys[...]) + mm(query_rot, rotary)) * score_scale
+        masked = jnp.where(visible, scores, neg_large)
+        top = jnp.max(masked, axis=1, keepdims=True)
+        weights = jnp.where(visible, jnp.exp(masked - top), 0.0)
+        whole = jnp.sum(weights, axis=1, keepdims=True)
+        update = lax.dot_general(
+            weights.astype(bf16), keys[...], (((1,), (1,)), ((), ())), preferred_element_type=f32
+        )
+        attn[:, pl.ds(pl.multiple_of(head * value, value), value)] = mm(
+            (update / whole).astype(bf16), uv[head]
+        ).astype(bf16)
+
+    for copy in local_attention():
+        copy.start()
+    ropes[0, turn:, :] = jnp.zeros((turn, ropes.shape[2]), bf16)
+    ropes[1, :turn, :] = jnp.zeros((turn, ropes.shape[2]), bf16)
+    for expert in range(nz):
+        line = jnp.zeros((1, table.shape[2]), f32)
+        for k in range(ids_ref.shape[0]):
+            line = line + jnp.where(
+                ids_ref[k : k + 1, :] == expert, scale_ref[k : k + 1, :], 0.0
+            )
+        table[expert] = jnp.broadcast_to(line, table.shape[1:])
     pl.semaphore_wait(barrier, nz + 1)
     for k in range(2):
         own_weights(k).start()
-    for i in range(chunks):
+    for i in range(half):
 
         @pl.when(z < last)
         def _():
@@ -438,23 +512,45 @@
         def _():
             give_rows(i, False).start()
 
-    for step in range(1, nz):
-        give_routes(step).start()
+    def give_rest(to_right):
+        for i in range(half, chunks):
+            give_rows(i, to_right).start()
+
+    @pl.when(z == 0)
+    def _():
+        give_rest(True)
+
+    @pl.when(z == last)
+    def _():
+        give_rest(False)
+
+    for copy in give_keys():
+        copy.start()
     for k in range(2):
         give_weights(k).start()
     own_weights(2).start()
     give_weights(2).start()
     for i in range(chunks):
         own_rows(i).start()
-    routes[z] = route_ref[z]
+    routes[z] = table[z]
+    for step in range(1, nz):
+        give_routes(step).start()
 
     row_group = lax.broadcasted_iota(jnp.int32, (rows, 128), 0) // 8
     lane = lax.broadcasted_iota(jnp.int32, (rows, 128), 1)
     block = fh if width % fh == 0 else 128
 
-    def spread(packed, offset):
+    def spread(packed):
         tall = jnp.broadcast_to(packed[None], (groups, 8, 128)).reshape(rows, 128)
-        return jnp.sum(jnp.where(lane == row_group + offset, tall, 0.0), axis=1, keepdims=True)
+        return jnp.sum(jnp.where(lane == row_group, tall, 0.0), axis=1, keepdims=True)
+
+    def weights_of(source, i):
+        tokens = routes.shape[2]
+        shape = (rows, tokens)
+        wanted = lax.broadcasted_iota(jnp.int32, shape, 0) + i * rows
+        hit = lax.broadcasted_iota(jnp.int32, shape, 1) == wanted
+        line = jnp.broadcast_to(routes[source][0:1, :], shape)
+        return jnp.sum(jnp.where(hit, line, 0.0), axis=1, keepdims=True)
 
     def exchange(at, slot):
         return (
@@ -466,7 +562,7 @@
         def normalise(n, total):
             cols = pl.ds(pl.multiple_of(n * block, block), block)
             wide = xs[at, :, cols].astype(f32)
-            scaled[:, cols] = (wide * gain_ref[:, cols]).astype(bf16)
+            scaled[:, cols] = (wide * gain_ref[cols][None, :]).astype(bf16)
             square = wide * wide
             for m in range(block // 128):
                 total = total + square[:, m * 128 : (m + 1) * 128]
@@ -489,8 +585,8 @@
     def expand(source, i, at, slot):
         for copy in exchange(at, slot):
             copy.wait()
-        scale = lax.rsqrt(spread(squares[slot] + squares_in[at], 0) / total_width + norm_eps)
-        weight = spread(routes[source], i * groups)
+        scale = lax.rsqrt(spread(squares[slot] + squares_in[at]) / total_width + norm_eps)
+        weight = weights_of(source, i)
 
         @pl.loop(0, 2)
         def _(b):
@@ -506,11 +602,23 @@
                 scaled[:, : 2 * fh], wd[:, cols], preferred_element_type=f32
             ).astype(bf16)
 
+    def arrival(k, from_left):
+        near = z if from_left else last - z
+        part = k // half
+        late = part >= near
+        source = jnp.where(late, part - near, near - 1 - part)
+        i = lax.rem(k, half) + jnp.where(late, half, 0)
+        there = (k >= 0) & (k < near * chunks)
+        return source if from_left else last - source, i, there
+
     def place(t, q):
-        hop, i = t // chunks, lax.rem(t, chunks)
-        source = jnp.where(q == 0, z - 1 - hop, jnp.where(q == 1, z + 1 + hop, z))
-        there = (t >= 0) & (t < spans) & (source >= 0) & (source <= last)
-        there = there & ((q < 2) | (hop == last - 1))
+        left_source, left_i, left_there = arrival(t, True)
+        right_source, right_i, right_there = arrival(t, False)
+        own_i = t - (spans - chunks)
+        own_there = (own_i >= 0) & (own_i < chunks)
+        source = jnp.where(q == 0, left_source, jnp.where(q == 1, right_source, z))
+        i = jnp.where(q == 0, left_i, jnp.where(q == 1, right_i, own_i))
+        there = ((q == 0) & left_there) | ((q == 1) & right_there) | ((q == 2) & own_there)
         return source, i, there
 
     def give_back(source, i, to_left):
@@ -536,22 +644,11 @@
                 value = value + ret[to, :, cols].astype(f32)
             con[at, :, cols] = value.astype(bf16)
 
-    def event(k, near):
-        kept = jnp.maximum(near - 1 - SLACK, 0)
-        first = chunks - kept
-        rest = k - first
-        is_first = k < first
-        is_mid = rest < (near - 1) * chunks
-        hop = jnp.where(is_first, 0, jnp.where(is_mid, 1 + rest // chunks, 0))
-        i = jnp.where(
-            is_first, k, jnp.where(is_mid, lax.rem(rest, chunks), first + rest - (near - 1) * chunks)
-        )
-        return hop, i
-
     def slot_step(t, carry):
-        for q, to_right in ((0, True), (1, False)):
-            source, i, there = place(t, q)
+        for to_right in (True, False):
+            source, i, there = arrival(t, to_right)
             onward = (z < last) if to_right else (z > 0)
+            near = z if to_right else last - z
 
             @pl.when(there)
             def _():
@@ -562,18 +659,9 @@
                 def _():
                     pass_rows(at, to_right).start()
 
-        for to_left in (True, False):
-            near = z if to_left else last - z
-            k = t + 1 - (nz - near) * chunks
-            go = (k >= 0) & (k < near * chunks) & (near < last)
-
-            @pl.when(go)
+            @pl.when(onward & (near > 0) & (t == near * chunks - 1))
             def _():
-                hop, i = event(k, near)
-                source = z - 1 - hop if to_left else z + 1 + hop
-                to = await_back(source, i, to_left)
-                add_back(source, i, [to])
-                give_back(source, i, to_left).start()
+                give_rest(to_right)
 
         @pl.when(t == 0)
         def _():
@@ -596,6 +684,23 @@
             for step in range(1, nz):
                 await_routes(step)
 
+        heads = uv.shape[0]
+
+        @pl.when(t == chunks)
+        def _():
+            for copy in local_attention():
+                copy.wait()
+            for copy in give_keys():
+                copy.wait()
+
+        @pl.when((t >= chunks) & (t < chunks + heads))
+        def _():
+            attend(t - chunks)
+
+        @pl.when(t == chunks + heads)
+        def _():
+            put_attention().start()
+
         @pl.loop(0, 3)
         def _(q):
             source, i, there = place(t - 1, q)
@@ -606,21 +711,20 @@
 
         for to_left in (True, False):
             near = z if to_left else last - z
-            source, i, there = place(t - 1, 0 if to_left else 1)
-            kept = jnp.maximum(near - 1 - SLACK, 0)
-            held = (t - 1 < chunks) & (i >= chunks - kept)
-
-            @pl.when(there & (near == last) & jnp.logical_not(held))
+            source, i, there = arrival(t - 1, to_left)
+
+            @pl.when(there & (near == last))
             def _():
                 give_back(source, i, to_left).start()
 
-            @pl.when((near == last) & (t == spans + 1))
+            k = t + half - (nz - near) * chunks
+            source_back, i_back, there_back = arrival(k, to_left)
+
+            @pl.when(there_back & (near < last))
             def _():
-                for n in range(chunks):
-
-                    @pl.when(n >= chunks - kept)
-                    def _():
-                        give_back(z - 1 if to_left else z + 1, n, to_left).start()
+                to = await_back(source_back, i_back, to_left)
+                add_back(source_back, i_back, [to])
+                give_back(source_back, i_back, to_left).start()
 
         return carry
 
@@ -648,6 +752,7 @@
     for i in range(chunks):
         finish(i).start()
 
+    put_attention().wait()
     for i in range(chunks):
         at = z * chunks + i
         pltpu.make_async_copy(
@@ -666,8 +771,8 @@
         give_routes(step).wait_send()
 
     def settle(t, carry):
-        for q, to_right in ((0, True), (1, False)):
-            source, i, there = place(t, q)
+        for to_right in (True, False):
+            source, i, there = arrival(t, to_right)
             onward = (z < last) if to_right else (z > 0)
 
             @pl.when(there)
@@ -683,10 +788,16 @@
     lax.fori_loop(0, spans, settle, 0)
 
 
-def expert_scratch(nz, rows, width, fh):
+def expert_scratch(nz, rows, width, fh, seq, heads, latent, turn, value, tokens):
     jobs = nz * CHUNKS
     dma = pltpu.SemaphoreType.DMA
     return [
+        pltpu.VMEM((seq, heads * latent), bf16),
+        pltpu.VMEM((seq, heads * turn), bf16),
+        pltpu.VMEM((latent, 2 * seq), bf16),
+        pltpu.VMEM((2, 2 * turn, 2 * seq), bf16),
+        pltpu.VMEM((heads, latent, value), bf16),
+        pltpu.VMEM((seq, heads * value), bf16),
         pltpu.VMEM((jobs, rows, width), bf16),
         pltpu.VMEM((4, width, fh), bf16),
         pltpu.VMEM((2 * fh, width), bf16),
@@ -698,7 +809,11 @@
         pltpu.VMEM((rows, width), bf16),
         pltpu.VMEM((6, 8, 128), f32),
         pltpu.VMEM((jobs, 8, 128), f32),
-        pltpu.VMEM((nz, 8, 128), f32),
+        pltpu.VMEM((nz, 8, tokens), f32),
+        pltpu.VMEM((nz, 8, tokens), f32),
+        dma((7,)),
+        dma((3,)),
+        dma((3,)),
         dma((3 + CHUNKS,)),
         dma((3,)),
         dma((3,)),
@@ -727,40 +842,53 @@
     return total
 
 
-def fits(moe_tokens, w_gate):
+def sizes(latent_keys, rope_keys, w_uv, moe_tokens, w_gate):
+    heads, latent, value = w_uv.shape
+    tokens, width = moe_tokens.shape
+    return dict(
+        nz=lax.axis_size("ep") // 2,
+        rows=tokens // CHUNKS,
+        width=width,
+        fh=w_gate.shape[2],
+        seq=latent_keys.shape[1],
+        heads=heads,
+        latent=latent,
+        turn=rope_keys.shape[0],
+        value=value,
+        tokens=tokens,
+    )
+
+
+def fits(n, w_gate):
     n_ep = lax.axis_size("ep")
-    nz = n_ep // 2
-    tokens, width = moe_tokens.shape
-    fh = w_gate.shape[2]
-    rows = tokens // CHUNKS
-    if lax.axis_size("ctx") != 2 or n_ep % 2 or nz < 2 or w_gate.shape[0] != 1:
+    if lax.axis_size("ctx") != 2 or n_ep % 2 or n["nz"] < 2 or w_gate.shape[0] != 1:
         return False
-    if tokens % (16 * CHUNKS) or tokens > 1024 or width % 128 or fh % 128:
+    if n["tokens"] % (16 * CHUNKS) or n["rows"] > 1024 or n["heads"] > (n["nz"] - 1) * CHUNKS:
         return False
-    return scratch_bytes(expert_scratch(nz, rows, width, fh)) < VMEM_BYTES - 2**21
-
-
-def experts(moe_tokens, norm_gain, expert_ids, route_scale, w_gate, w_up, w_down):
-    nz = lax.axis_size("ep") // 2
-    tokens, width = moe_tokens.shape
-    fh = w_gate.shape[2]
-    rows = tokens // CHUNKS
-    named = expert_ids[None] == jnp.arange(nz, dtype=jnp.int32)[:, None, None]
-    table = jnp.sum(jnp.where(named, route_scale[None], 0.0), axis=2)
-    table = table.reshape(nz, tokens // 8, 8).transpose(0, 2, 1)
-    table = jnp.pad(table, ((0, 0), (0, 0), (0, 128 - tokens // 8)))
+    lanes = ("width", "fh", "seq", "latent", "value", "tokens")
+    if any(n[name] % 128 for name in lanes) or n["turn"] != 64 or n["heads"] % 2:
+        return False
+    return scratch_bytes(expert_scratch(**n)) < VMEM_BYTES - 2**20
+
+
+def fused(n, attention_in, moe_in):
+    moe_tokens, norm_gain, expert_ids, route_scale, w_gate, w_up, w_down = moe_in
     anywhere = pl.BlockSpec(memory_space=pl.ANY)
     whole = pl.BlockSpec(memory_space=pltpu.VMEM)
+    total = n["width"] * lax.axis_size("ctx")
     return pl.pallas_call(
-        functools.partial(expert_kernel, nz, CHUNKS, width * lax.axis_size("ctx")),
-        out_shape=jax.ShapeDtypeStruct((tokens, width), bf16),
-        in_specs=[anywhere] * 4 + [whole] * 2,
-        out_specs=anywhere,
-        scratch_shapes=expert_scratch(nz, rows, width, fh),
+        functools.partial(expert_kernel, n["nz"], CHUNKS, total),
+        out_shape=(
+            jax.ShapeDtypeStruct((n["seq"], n["heads"] * n["value"]), bf16),
+            jax.ShapeDtypeStruct((n["tokens"], n["width"]), bf16),
+        ),
+        in_specs=[anywhere] * 9 + [whole] * 3,
+        out_specs=(anywhere, anywhere),
+        scratch_shapes=expert_scratch(**n),
         compiler_params=pltpu.CompilerParams(
             collective_id=0, has_side_effects=True, vmem_limit_bytes=VMEM_BYTES
         ),
-    )(moe_tokens, w_gate, w_up, w_down, norm_gain[None, :], table)
+    )(*attention_in, moe_tokens, w_gate, w_up, w_down, norm_gain, expert_ids.T, route_scale.T)
 
 
 def body(
@@ -777,7 +905,8 @@
     w_up,
     w_down,
 ):
-    if not fits(moe_tokens, w_gate):
+    n = sizes(latent_keys, rope_keys, w_uv, moe_tokens, w_gate)
+    if not fits(n, w_gate):
         return hop_body(
             q_latent,
             q_rope,
@@ -792,9 +921,9 @@
             w_up,
             w_down,
         )
-    moe_out = experts(moe_tokens, norm_gain, expert_ids, route_scale, w_gate, w_up, w_down)
-    attn_out = attention(q_latent, q_rope, latent_keys, rope_keys, w_uv)
-    return (attn_out, moe_out)
+    attention_in = (q_latent, q_rope, latent_keys, rope_keys, w_uv)
+    moe_in = (moe_tokens, norm_gain, expert_ids, route_scale, w_gate, w_up, w_down)
+    return fused(n, attention_in, moe_in)
 
 
 def solution(mesh):

time: 236 us -> 182 us (0.77)
  the two profiles are of different devices: /device:TPU:24 before, /device:TPU:0 now
where the time goes in v1:
time: 182 us; the launch traced here: 181 us
  Pallas kernels  176 us (97%)
  local copies, waits for them, and re-layouts  4.41 us (2%)
    pallas_call x1, Pallas kernels, fused(): pl.pallas_call(functools.partial(expert_kernel, n['nz'], CHUNKS, total),...  176 us
    unnamed x2, local copies, waits for them, and re-layouts  4.41 us

profile of v1, /device:TPU:0, one launch (start us, length us, event | category | flops | bytes accessed | tf_op | source)
XLA Modules:
  0.0 181.4 jit_solution(13247312154812163727)
XLA Ops:
  0.6 176.4 %shard_map.131 = (bf16[128,512]{1,0:T(8,128)(2,1)}, bf16[256,3584]{1,0:T(8,128)(2,1)}) custom-call(bf16[128,2048]{1,0:T(8,128)(2,1)} %ql_hbm.1, bf16[128,256]{1,0:T(8,128)(2,1)} %qr_hbm.1, bf16[512,128]{1,0:T(8,128)(2,1)} %lk_hbm.1, bf16[64,128]{1,0:T(8,128)(2,1)} %rk_hbm.1, bf16[4,512,128]{2,1,0:T(8,128)(2,1)} %uv_hbm.1, bf16[256,3584]{1,0:T(8,128)(2,1)} %x_hbm.1, ...), custom_call_target="tpu_custom_call" | custom-call | tf_op jit(solution)/shard_map/pallas_call | solution.py:879
  177.0 1.6 copy.16
  178.6 2.8 %copy.17 = bf16[256,3584]{1,0:T(8,128)(2,1)} copy(bf16[256,3584]{1,0:T(8,128)(2,1)} %get-tuple-element.5) | data formatting | bytes 3670016

commit v2 on v1

--- a/solution.py
+++ b/solution.py
@@ -11,6 +11,8 @@
 neg_large = -1e30
 PIECES = 2
 CHUNKS = 4
+LAG = 2
+STEPS = 2
 VMEM_BYTES = 67043328
 f32 = jnp.float32
 bf16 = jnp.bfloat16
@@ -319,7 +321,9 @@
     ids_ref,
     scale_ref,
     attn_hbm,
-    out_hbm,
+    own_hbm,
+    right_hbm,
+    left_hbm,
     ql,
     qr,
     keys,
@@ -337,7 +341,6 @@
     scaled,
     squares,
     squares_in,
-    table,
     routes,
     a_local,
     a_send,
@@ -382,13 +385,14 @@
         )
 
     barrier = pltpu.get_barrier_semaphore()
-    for step in range(1, nz):
-        pl.semaphore_signal(
-            barrier,
-            inc=1,
-            device_id={"ep": 2 * lax.rem(z + step, nz) + core},
-            device_id_type=pl.DeviceIdType.MESH,
-        )
+    for near, device in ((z > 0, left), (z < last, right)):
+
+        @pl.when(near)
+        def _():
+            pl.semaphore_signal(
+                barrier, inc=1, device_id=device, device_id_type=pl.DeviceIdType.MESH
+            )
+
     for device in (across, beside):
         pl.semaphore_signal(
             barrier, inc=1, device_id=device, device_id_type=pl.DeviceIdType.MESH
@@ -415,7 +419,7 @@
         side = right if to_right else left
         sem = z * chunks + i if to_right else nz * chunks + i
         return remote(
-            x_hbm.at[pl.ds(i * rows, rows), :],
+            xs.at[z * chunks + i],
             xs.at[z * chunks + i],
             x_send.at[sem],
             x_recv.at[z * chunks + i],
@@ -426,21 +430,15 @@
         side = right if to_right else left
         return remote(xs.at[at], xs.at[at], x_send.at[at], x_recv.at[at], side)
 
-    def give_routes(step):
-        to = lax.rem(z + step, nz)
+    def pass_routes(source, to_right):
+        side = right if to_right else left
         return remote(
-            table.at[to],
-            routes.at[z],
-            t_send.at[to],
-            t_recv.at[z],
-            {"ep": 2 * to + core},
+            routes.at[source],
+            routes.at[source],
+            t_send.at[source if to_right else source + 1],
+            t_recv.at[source],
+            side,
         )
-
-    def await_routes(step):
-        of = lax.rem(z + step, nz)
-        remote(
-            table.at[of], routes.at[of], t_send.at[of], t_recv.at[of], {"ep": 2 * of + core}
-        ).wait_recv()
 
     seq = ql.shape[0]
     latent = keys.shape[0]
@@ -488,21 +486,37 @@
             (update / whole).astype(bf16), uv[head]
         ).astype(bf16)
 
-    for copy in local_attention():
-        copy.start()
+    for i in range(chunks):
+        own_rows(i).start()
+
     ropes[0, turn:, :] = jnp.zeros((turn, ropes.shape[2]), bf16)
     ropes[1, :turn, :] = jnp.zeros((turn, ropes.shape[2]), bf16)
     for expert in range(nz):
-        line = jnp.zeros((1, table.shape[2]), f32)
+        line = jnp.zeros((1, routes.shape[3]), f32)
         for k in range(ids_ref.shape[0]):
             line = line + jnp.where(
                 ids_ref[k : k + 1, :] == expert, scale_ref[k : k + 1, :], 0.0
             )
-        table[expert] = jnp.broadcast_to(line, table.shape[1:])
-    pl.semaphore_wait(barrier, nz + 1)
-    for k in range(2):
-        own_weights(k).start()
+        routes[z, expert] = line
+
+    @pl.when((z == 0) | (z == last))
+    def _():
+        pl.semaphore_wait(barrier, 3)
+
+    @pl.when((z > 0) & (z < last))
+    def _():
+        pl.semaphore_wait(barrier, 4)
+
+    @pl.when(z < last)
+    def _():
+        pass_routes(z, True).start()
+
+    @pl.when(z > 0)
+    def _():
+        pass_routes(z, False).start()
+
     for i in range(half):
+        own_rows(i).wait()
 
         @pl.when(z < last)
         def _():
@@ -516,6 +530,11 @@
         for i in range(half, chunks):
             give_rows(i, to_right).start()
 
+    for k in range(2):
+        own_weights(k).start()
+    for i in range(half, chunks):
+        own_rows(i).wait()
+
     @pl.when(z == 0)
     def _():
         give_rest(True)
@@ -524,18 +543,12 @@
     def _():
         give_rest(False)
 
-    for copy in give_keys():
+    for copy in local_attention() + give_keys():
         copy.start()
     for k in range(2):
         give_weights(k).start()
     own_weights(2).start()
     give_weights(2).start()
-    for i in range(chunks):
-        own_rows(i).start()
-    routes[z] = table[z]
-    for step in range(1, nz):
-        give_routes(step).start()
-
     row_group = lax.broadcasted_iota(jnp.int32, (rows, 128), 0) // 8
     lane = lax.broadcasted_iota(jnp.int32, (rows, 128), 1)
     block = fh if width % fh == 0 else 128
@@ -545,62 +558,103 @@
         return jnp.sum(jnp.where(lane == row_group, tall, 0.0), axis=1, keepdims=True)
 
     def weights_of(source, i):
-        tokens = routes.shape[2]
+        tokens = routes.shape[3]
         shape = (rows, tokens)
         wanted = lax.broadcasted_iota(jnp.int32, shape, 0) + i * rows
         hit = lax.broadcasted_iota(jnp.int32, shape, 1) == wanted
-        line = jnp.broadcast_to(routes[source][0:1, :], shape)
+        line = jnp.broadcast_to(routes[source, z], shape)
         return jnp.sum(jnp.where(hit, line, 0.0), axis=1, keepdims=True)
 
-    def exchange(at, slot):
+    def exchange(at, slot, lane_at):
         return (
-            remote(outgoing.at[slot], theirs.at[at], p_send.at[at], p_recv.at[at], across),
-            remote(squares.at[slot], squares_in.at[at], q_send.at[at], q_recv.at[at], across),
+            remote(
+                outgoing.at[slot, lane_at], theirs.at[at], p_send.at[at], p_recv.at[at], across
+            ),
+            remote(
+                squares.at[slot, lane_at], squares_in.at[at], q_send.at[at], q_recv.at[at], across
+            ),
         )
 
-    def project(at, slot):
-        def normalise(n, total):
+    def normalise(at, slot, lane_at):
+        lines = pl.ds(lane_at * rows, rows)
+
+        def columns(n, total):
             cols = pl.ds(pl.multiple_of(n * block, block), block)
             wide = xs[at, :, cols].astype(f32)
-            scaled[:, cols] = (wide * gain_ref[cols][None, :]).astype(bf16)
+            scaled[lines, cols] = (wide * gain_ref[cols][None, :]).astype(bf16)
             square = wide * wide
             for m in range(block // 128):
                 total = total + square[:, m * 128 : (m + 1) * 128]
             return total
 
-        total = lax.fori_loop(0, width // block, normalise, jnp.zeros((rows, 128), f32))
+        total = lax.fori_loop(0, width // block, columns, jnp.zeros((rows, 128), f32))
         column = jnp.sum(total, axis=1, keepdims=True)
         packed = jnp.where(lane == row_group, jnp.broadcast_to(column, (rows, 128)), 0.0)
-        squares[slot] = jnp.sum(packed.reshape(groups, 8, 128), axis=0)
-
-        @pl.loop(0, 4)
-        def _(k):
-            part = jnp.dot(scaled[...], wgu[k], preferred_element_type=f32)
-            mine[slot, k] = part
-            outgoing[slot, k] = part.astype(bf16)
-
-        for copy in exchange(at, slot):
-            copy.start()
-
-    def expand(source, i, at, slot):
-        for copy in exchange(at, slot):
+        squares[slot, lane_at] = jnp.sum(packed.reshape(groups, 8, 128), axis=0)
+
+    def project(t):
+        slot = lax.rem(t, LAG + 1)
+        places = [place(t, n) for n in range(2)]
+        for n, (source, i, there) in enumerate(places):
+
+            @pl.when(there)
+            def _():
+                normalise(source * chunks + i, slot, n)
+
+        @pl.when(places[0][2] | places[1][2])
+        def _():
+            @pl.loop(0, 4)
+            def _(k):
+                part = jnp.dot(scaled[...], wgu[k], preferred_element_type=f32)
+                mine[slot, k] = part
+                for n in range(2):
+                    outgoing[slot, n, k] = part[n * rows : (n + 1) * rows].astype(bf16)
+
+        for n, (source, i, there) in enumerate(places):
+
+            @pl.when(there)
+            def _():
+                for copy in exchange(source * chunks + i, slot, n):
+                    copy.start()
+
+    def activate(source, i, slot, lane_at):
+        at = source * chunks + i
+        lines = pl.ds(lane_at * rows, rows)
+        for copy in exchange(at, slot, lane_at):
             copy.wait()
-        scale = lax.rsqrt(spread(squares[slot] + squares_in[at]) / total_width + norm_eps)
+        square = spread(squares[slot, lane_at] + squares_in[at])
+        scale = lax.rsqrt(square / total_width + norm_eps)
         weight = weights_of(source, i)
 
         @pl.loop(0, 2)
         def _(b):
-            gate = (mine[slot, b] + theirs[at, b].astype(f32)) * scale
-            up = (mine[slot, b + 2] + theirs[at, b + 2].astype(f32)) * scale
+            gate = (mine[slot, b, lines] + theirs[at, b].astype(f32)) * scale
+            up = (mine[slot, b + 2, lines] + theirs[at, b + 2].astype(f32)) * scale
             hid = jax.nn.silu(gate) * up * weight
-            scaled[:, pl.ds(pl.multiple_of(b * fh, fh), fh)] = hid.astype(bf16)
-
-        @pl.loop(0, width // block)
-        def _(n):
-            cols = pl.ds(pl.multiple_of(n * block, block), block)
-            con[at, :, cols] = jnp.dot(
-                scaled[:, : 2 * fh], wd[:, cols], preferred_element_type=f32
-            ).astype(bf16)
+            scaled[lines, pl.ds(pl.multiple_of(b * fh, fh), fh)] = hid.astype(bf16)
+
+    def expand(t):
+        slot = lax.rem(t + LAG + 1, LAG + 1)
+        places = [place(t, n) for n in range(2)]
+        for n, (source, i, there) in enumerate(places):
+
+            @pl.when(there)
+            def _():
+                activate(source, i, slot, n)
+
+        @pl.when(places[0][2] | places[1][2])
+        def _():
+            @pl.loop(0, width // block)
+            def _(b):
+                cols = pl.ds(pl.multiple_of(b * block, block), block)
+                part = jnp.dot(scaled[:, : 2 * fh], wd[:, cols], preferred_element_type=f32)
+                for n, (source, i, there) in enumerate(places):
+
+                    @pl.when(there)
+                    def _():
+                        con[source * chunks + i, :, cols] = part[
+                            n * rows : (n + 1) * rows
+                        ].astype(bf16)
 
     def arrival(k, from_left):
         near = z if from_left else last - z
@@ -611,21 +665,36 @@
         there = (k >= 0) & (k < near * chunks)
         return source if from_left else last - source, i, there
 
-    def place(t, q):
-        left_source, left_i, left_there = arrival(t, True)
-        right_source, right_i, right_there = arrival(t, False)
+    def place(t, lane_at):
+        source, i, there = arrival(t, lane_at == 0)
         own_i = t - (spans - chunks)
-        own_there = (own_i >= 0) & (own_i < chunks)
-        source = jnp.where(q == 0, left_source, jnp.where(q == 1, right_source, z))
-        i = jnp.where(q == 0, left_i, jnp.where(q == 1, right_i, own_i))
-        there = ((q == 0) & left_there) | ((q == 1) & right_there) | ((q == 2) & own_there)
-        return source, i, there
-
-    def give_back(source, i, to_left):
+        own = (own_i >= 0) & (own_i < chunks)
+        own = own & ((z < last) if lane_at == 0 else (z == last))
+        own = own & jnp.logical_not(there)
+        return jnp.where(own, z, source), jnp.where(own, own_i, i), there | own
+
+    def give_back(source, i, to_left, home=False):
         at = source * chunks + i
         to = at if to_left else at + chunks
         side = left if to_left else right
-        return remote(con.at[at], ret.at[to], r_send.at[at], r_recv.at[to], side)
+        lines = pl.ds(pl.multiple_of(i * rows, rows), rows)
+        dst = (right_hbm if to_left else left_hbm).at[lines] if home else ret.at[to]
+        return remote(con.at[at], dst, r_send.at[at], r_recv.at[to], side)
+
+    def send_back(source, i, to_left):
+        is_home = source == (z - 1 if to_left else z + 1)
+
+        @pl.when(is_home)
+        def _():
+            give_back(source, i, to_left, True).start()
+
+        @pl.when(jnp.logical_not(is_home))
+        def _():
+            give_back(source, i, to_left).start()
+
+    def put_own(i):
+        lines = pl.ds(pl.multiple_of(i * rows, rows), rows)
+        return pltpu.make_async_copy(con.at[z * chunks + i], own_hbm.at[lines], o_sem.at[i])
 
     def await_back(source, i, to_left):
         at = source * chunks + i
@@ -659,6 +728,14 @@
                 def _():
                     pass_rows(at, to_right).start()
 
+                @pl.when(i == 0)
+                def _():
+                    pass_routes(source, to_right).wait_recv()
+
+                    @pl.when(onward)
+                    def _():
+                        pass_routes(source, to_right).start()
+
             @pl.when(onward & (near > 0) & (t == near * chunks - 1))
             def _():
                 give_rest(to_right)
@@ -669,20 +746,12 @@
                 own_weights(k).wait()
                 give_weights(k).wait()
 
-        @pl.loop(0, 3)
-        def _(q):
-            source, i, there = place(t, q)
-
-            @pl.when(there)
-            def _():
-                project(source * chunks + i, lax.rem(t, 2) * 3 + q)
-
-        @pl.when(t == 1)
+        project(t)
+
+        @pl.when(t == LAG)
         def _():
             own_weights(2).wait()
             give_weights(2).wait()
-            for step in range(1, nz):
-                await_routes(step)
 
         heads = uv.shape[0]
 
@@ -701,21 +770,21 @@
         def _():
             put_attention().start()
 
-        @pl.loop(0, 3)
-        def _(q):
-            source, i, there = place(t - 1, q)
-
-            @pl.when(there)
-            def _():
-                expand(source, i, source * chunks + i, lax.rem(t + 1, 2) * 3 + q)
+        expand(t - LAG)
+
+        own_i = t - LAG - (spans - chunks)
+
+        @pl.when((own_i >= 0) & (own_i < chunks))
+        def _():
+            put_own(own_i).start()
 
         for to_left in (True, False):
             near = z if to_left else last - z
-            source, i, there = arrival(t - 1, to_left)
+            source, i, there = arrival(t - LAG, to_left)
 
             @pl.when(there & (near == last))
             def _():
-                give_back(source, i, to_left).start()
+                send_back(source, i, to_left)
 
             k = t + half - (nz - near) * chunks
             source_back, i_back, there_back = arrival(k, to_left)
@@ -724,40 +793,25 @@
             def _():
                 to = await_back(source_back, i_back, to_left)
                 add_back(source_back, i_back, [to])
-                give_back(source_back, i_back, to_left).start()
+                send_back(source_back, i_back, to_left)
 
         return carry
 
+    lax.fori_loop(0, nz * chunks, slot_step, 0)
+
     for i in range(chunks):
-        own_rows(i).wait()
-    lax.fori_loop(0, nz * chunks, slot_step, 0)
-
-    def finish(i):
-        at = z * chunks + i
+        put_own(i).wait()
 
         @pl.when(z < last)
         def _():
-            to = await_back(z, i, True)
-            add_back(z, i, [to])
+            give_back(z, i, True, True).wait_recv()
 
         @pl.when(z > 0)
         def _():
-            to = await_back(z, i, False)
-            add_back(z, i, [to])
-
-        return pltpu.make_async_copy(
-            con.at[at], out_hbm.at[pl.ds(i * rows, rows), :], o_sem.at[i]
-        )
-
-    for i in range(chunks):
-        finish(i).start()
+            give_back(z, i, False, True).wait_recv()
 
     put_attention().wait()
     for i in range(chunks):
-        at = z * chunks + i
-        pltpu.make_async_copy(
-            con.at[at], out_hbm.at[pl.ds(i * rows, rows), :], o_sem.at[i]
-        ).wait()
 
         @pl.when(z < last)
         def _():
@@ -767,8 +821,13 @@
         def _():
             give_rows(i, False).wait_send()
 
-    for step in range(1, nz):
-        give_routes(step).wait_send()
+    @pl.when(z < last)
+    def _():
+        pass_routes(z, True).wait_send()
+
+    @pl.when(z > 0)
+    def _():
+        pass_routes(z, False).wait_send()
 
     def settle(t, carry):
         for to_right in (True, False):
@@ -783,9 +842,22 @@
                 def _():
                     pass_rows(source * chunks + i, to_right).wait_send()
 
+                @pl.when(onward & (i == 0))
+                def _():
+                    pass_routes(source, to_right).wait_send()
+
         return carry
 
     lax.fori_loop(0, spans, settle, 0)
+
+
+def gather_kernel(last, attn_in, own_ref, right_ref, left_ref, attn_out, out_ref):
+    z = lax.axis_index("ep") // 2
+    attn_out[...] = attn_in[...]
+    value = own_ref[...].astype(f32)
+    value = value + jnp.where(z < last, right_ref[...].astype(f32), 0.0)
+    value = value + jnp.where(z > 0, left_ref[...].astype(f32), 0.0)
+    out_ref[...] = value.astype(bf16)
 
 
 def expert_scratch(nz, rows, width, fh, seq, heads, latent, turn, value, tokens):
@@ -804,13 +876,12 @@
         pltpu.VMEM((jobs + CHUNKS, rows, width), bf16),
         pltpu.VMEM((jobs, rows, width), bf16),
         pltpu.VMEM((jobs, 4, rows, fh), bf16),
-        pltpu.VMEM((6, 4, rows, fh), f32),
-        pltpu.VMEM((6, 4, rows, fh), bf16),
-        pltpu.VMEM((rows, width), bf16),
-        pltpu.VMEM((6, 8, 128), f32),
+        pltpu.VMEM((LAG + 1, 4, 2 * rows, fh), f32),
+        pltpu.VMEM((LAG + 1, 2, 4, rows, fh), bf16),
+        pltpu.VMEM((2 * rows, width), bf16),
+        pltpu.VMEM((LAG + 1, 2, 8, 128), f32),
         pltpu.VMEM((jobs, 8, 128), f32),
-        pltpu.VMEM((nz, 8, tokens), f32),
-        pltpu.VMEM((nz, 8, tokens), f32),
+        pltpu.VMEM((nz, nz, 1, tokens), f32),
         dma((7,)),
         dma((3,)),
         dma((3,)),
@@ -825,7 +896,7 @@
         dma((jobs,)),
         dma((jobs,)),
         dma((jobs,)),
-        dma((nz,)),
+        dma((nz + 1,)),
         dma((nz,)),
         dma((CHUNKS,)),
     ]
@@ -876,19 +947,28 @@
     anywhere = pl.BlockSpec(memory_space=pl.ANY)
     whole = pl.BlockSpec(memory_space=pltpu.VMEM)
     total = n["width"] * lax.axis_size("ctx")
-    return pl.pallas_call(
+    attn_shape = jax.ShapeDtypeStruct((n["seq"], n["heads"] * n["value"]), bf16)
+    rows_shape = jax.ShapeDtypeStruct((n["tokens"], n["width"]), bf16)
+    parts = pl.pallas_call(
         functools.partial(expert_kernel, n["nz"], CHUNKS, total),
-        out_shape=(
-            jax.ShapeDtypeStruct((n["seq"], n["heads"] * n["value"]), bf16),
-            jax.ShapeDtypeStruct((n["tokens"], n["width"]), bf16),
-        ),
+        out_shape=(attn_shape, rows_shape, rows_shape, rows_shape),
         in_specs=[anywhere] * 9 + [whole] * 3,
-        out_specs=(anywhere, anywhere),
+        out_specs=(anywhere,) * 4,
         scratch_shapes=expert_scratch(**n),
         compiler_params=pltpu.CompilerParams(
             collective_id=0, has_side_effects=True, vmem_limit_bytes=VMEM_BYTES
         ),
     )(*attention_in, moe_tokens, w_gate, w_up, w_down, norm_gain, expert_ids.T, route_scale.T)
+    steps = STEPS if n["seq"] % (16 * STEPS) == 0 and n["tokens"] % (16 * STEPS) == 0 else 1
+    attn_block = pl.BlockSpec((n["seq"] // steps, attn_shape.shape[1]), lambda i: (i, 0))
+    rows_block = pl.BlockSpec((n["tokens"] // steps, n["width"]), lambda i: (i, 0))
+    return pl.pallas_call(
+        functools.partial(gather_kernel, n["nz"] - 1),
+        grid=(steps,),
+        out_shape=(attn_shape, rows_shape),
+        in_specs=[attn_block] + [rows_block] * 3,
+        out_specs=(attn_block, rows_block),
+    )(*parts)
 
 
 def body(

time: 182 us -> 170 us (0.934)
  Pallas kernels: 176 us -> 169 us
  local copies, waits for them, and re-layouts: 4.41 us -> 0 us
    pallas_call x1, Pallas kernels: 176 us -> 165 us  [fused(): pl.pallas_call(functools.partial(expert_kernel, n['nz'], CHUNKS, total),...]
    unnamed x2 -> x0, local copies, waits for them, and re-layouts: 4.41 us -> none
    pallas_call x0 -> x1, Pallas kernels: none -> 4.01 us  [fused(): pl.pallas_call(functools.partial(gather_kernel, n['nz'] - 1), grid=(steps...]
where the time goes in v2:
time: 170 us
  Pallas kernels  169 us (99%)
    pallas_call x1, Pallas kernels, fused(): pl.pallas_call(functools.partial(expert_kernel, n['nz'], CHUNKS, total),...  165 us
    pallas_call x1, Pallas kernels, fused(): pl.pallas_call(functools.partial(gather_kernel, n['nz'] - 1), grid=(steps...  4.01 us

profile of v2, /device:TPU:0, one launch (start us, length us, event | category | flops | bytes accessed | tf_op | source)
XLA Modules:
  0.0 170.0 jit_solution(4942235535138953103)
XLA Ops:
  0.6 165.3 %shard_map.131 = (bf16[128,512]{1,0:T(8,128)(2,1)}, bf16[256,3584]{1,0:T(8,128)(2,1)}, bf16[256,3584]{1,0:T(8,128)(2,1)}, bf16[256,3584]{1,0:T(8,128)(2,1)}) custom-call(bf16[128,2048]{1,0:T(8,128)(2,1)} %ql_hbm.1, bf16[128,256]{1,0:T(8,128)(2,1)} %qr_hbm.1, bf16[512,128]{1,0:T(8,128)(2,1)} %lk_hbm.1, bf16[64,128]{1,0:T(8,128)(2,1)} %rk_hbm.1, ...), custom_call_target="tpu_custom_call" | custom-call | tf_op jit(solution)/shard_map/pallas_call | solution.py:952
  166.0 4.0 %shard_map.132 = (bf16[128,512]{1,0:T(8,128)(2,1)}, bf16[256,3584]{1,0:T(8,128)(2,1)}) custom-call(bf16[128,512]{1,0:T(8,128)(2,1)} %get-tuple-element.6.attn_in, bf16[256,3584]{1,0:T(8,128)(2,1)} %get-tuple-element.7.own_ref, bf16[256,3584]{1,0:T(8,128)(2,1)} %get-tuple-element.8.right_ref, bf16[256,3584]{1,0:T(8,128)(2,1)} %get-tuple-element.9.left_ref), custom_call_target="tpu_custom_call" | custom-call | tf_op jit(solution)/shard_map/pallas_call | solution.py:965

commit v3 on v2

--- a/solution.py
+++ b/solution.py
@@ -12,7 +12,6 @@
 PIECES = 2
 CHUNKS = 4
 LAG = 2
-STEPS = 2
 VMEM_BYTES = 67043328
 f32 = jnp.float32
 bf16 = jnp.bfloat16
@@ -317,13 +316,16 @@
     wg_hbm,
     wu_hbm,
     wd_hbm,
-    gain_ref,
-    ids_ref,
-    scale_ref,
+    gain_hbm,
+    ids_hbm,
+    scale_hbm,
     attn_hbm,
     own_hbm,
     right_hbm,
     left_hbm,
+    gain_ref,
+    ids_ref,
+    scale_ref,
     ql,
     qr,
     keys,
@@ -359,6 +361,7 @@
     t_send,
     t_recv,
     o_sem,
+    s_sem,
 ):
     ep = lax.axis_index("ep")
     z = ep // 2
@@ -489,8 +492,18 @@
     for i in range(chunks):
         own_rows(i).start()
 
+    small = [
+        pltpu.make_async_copy(src, dst, s_sem.at[n])
+        for n, (src, dst) in enumerate(
+            ((ids_hbm, ids_ref), (scale_hbm, scale_ref), (gain_hbm, gain_ref))
+        )
+    ]
+    for copy in small:
+        copy.start()
     ropes[0, turn:, :] = jnp.zeros((turn, ropes.shape[2]), bf16)
     ropes[1, :turn, :] = jnp.zeros((turn, ropes.shape[2]), bf16)
+    for copy in small:
+        copy.wait()
     for expert in range(nz):
         line = jnp.zeros((1, routes.shape[3]), f32)
         for k in range(ids_ref.shape[0]):
@@ -677,12 +690,11 @@
         at = source * chunks + i
         to = at if to_left else at + chunks
         side = left if to_left else right
-        lines = pl.ds(pl.multiple_of(i * rows, rows), rows)
-        dst = (right_hbm if to_left else left_hbm).at[lines] if home else ret.at[to]
+        dst = (right_hbm if to_left else left_hbm) if home else ret.at[to]
         return remote(con.at[at], dst, r_send.at[at], r_recv.at[to], side)
 
     def send_back(source, i, to_left):
-        is_home = source == (z - 1 if to_left else z + 1)
+        is_home = (source == (z - 1 if to_left else z + 1)) & (i == chunks - 1)
 
         @pl.when(is_home)
         def _():
@@ -772,11 +784,9 @@
 
         expand(t - LAG)
 
-        own_i = t - LAG - (spans - chunks)
-
-        @pl.when((own_i >= 0) & (own_i < chunks))
-        def _():
-            put_own(own_i).start()
+        @pl.when(t - LAG == spans - 1)
+        def _():
+            put_own(chunks - 1).start()
 
         for to_left in (True, False):
             near = z if to_left else last - z
@@ -799,16 +809,18 @@
 
     lax.fori_loop(0, nz * chunks, slot_step, 0)
 
-    for i in range(chunks):
-        put_own(i).wait()
-
-        @pl.when(z < last)
-        def _():
-            give_back(z, i, True, True).wait_recv()
-
-        @pl.when(z > 0)
-        def _():
-            give_back(z, i, False, True).wait_recv()
+    for where, sides in (
+        (z == 0, (True,)),
+        (z == last, (False,)),
+        ((z > 0) & (z < last), (True, False)),
+    ):
+
+        @pl.when(where)
+        def _():
+            @pl.loop(0, chunks - 1)
+            def _(i):
+                add_back(z, i, [await_back(z, i, to_left) for to_left in sides])
+                put_own(i).start()
 
     put_attention().wait()
     for i in range(chunks):
@@ -850,20 +862,85 @@
 
     lax.fori_loop(0, spans, settle, 0)
 
-
-def gather_kernel(last, attn_in, own_ref, right_ref, left_ref, attn_out, out_ref):
+    for i in range(chunks):
+        put_own(i).wait()
+
+    @pl.when(z < last)
+    def _():
+        give_back(z, chunks - 1, True, True).wait_recv()
+
+    @pl.when(z > 0)
+    def _():
+        give_back(z, chunks - 1, False, True).wait_recv()
+
+
+def gather_kernel(
+    last,
+    chunks,
+    attn_in,
+    own_in,
+    right_in,
+    left_in,
+    attn_out,
+    out_hbm,
+    attn,
+    own,
+    right,
+    left,
+    sem_in,
+    sem_out,
+):
     z = lax.axis_index("ep") // 2
-    attn_out[...] = attn_in[...]
-    value = own_ref[...].astype(f32)
-    value = value + jnp.where(z < last, right_ref[...].astype(f32), 0.0)
-    value = value + jnp.where(z > 0, left_ref[...].astype(f32), 0.0)
-    out_ref[...] = value.astype(bf16)
-
-
-def expert_scratch(nz, rows, width, fh, seq, heads, latent, turn, value, tokens):
+    rows, width = right.shape
+
+    def take(i):
+        return pltpu.make_async_copy(own_in.at[pl.ds(i * rows, rows)], own.at[i], sem_in.at[i])
+
+    def put(i):
+        return pltpu.make_async_copy(own.at[i], out_hbm.at[pl.ds(i * rows, rows)], sem_out.at[i])
+
+    final = chunks - 1
+    take_right = pltpu.make_async_copy(right_in, right, sem_in.at[chunks])
+    take_left = pltpu.make_async_copy(left_in, left, sem_in.at[chunks + 1])
+    take_attn = pltpu.make_async_copy(attn_in, attn, sem_in.at[chunks + 2])
+    put_attn = pltpu.make_async_copy(attn, attn_out, sem_out.at[chunks])
+    take(final).start()
+    take_right.start()
+    take_left.start()
+    take_attn.start()
+    for i in range(final):
+        take(i).start()
+    take(final).wait()
+    take_right.wait()
+    take_left.wait()
+    block = 512 if width % 512 == 0 else 128
+
+    @pl.loop(0, width // block)
+    def _(n):
+        cols = pl.ds(pl.multiple_of(n * block, block), block)
+        value = own[final, :, cols].astype(f32)
+        value = value + jnp.where(z < last, right[:, cols].astype(f32), 0.0)
+        value = value + jnp.where(z > 0, left[:, cols].astype(f32), 0.0)
+        own[final, :, cols] = value.astype(bf16)
+
+    put(final).start()
+    take_attn.wait()
+    put_attn.start()
+    for i in range(final):
+        take(i).wait()
+        put(i).start()
+    put_attn.wait()
+    for i in range(chunks):
+        put(i).wait()
+
+
+def expert_scratch(nz, rows, width, fh, seq, heads, latent, turn, value, tokens, top):
     jobs = nz * CHUNKS
     dma = pltpu.SemaphoreType.DMA
     return [
+        pltpu.VMEM((width,), f32),
+        pltpu.VMEM((top, tokens), jnp.int32),
+        pltpu.VMEM((top, tokens), f32),
         pltpu.VMEM((seq, heads * latent), bf16),
         pltpu.VMEM((seq, heads * turn), bf16),
         pltpu.VMEM((latent, 2 * seq), bf16),
@@ -899,6 +976,7 @@
         dma((nz + 1,)),
         dma((nz,)),
         dma((CHUNKS,)),
+        dma((3,)),
     ]
 
 
@@ -913,7 +991,7 @@
     return total
 
 
-def sizes(latent_keys, rope_keys, w_uv, moe_tokens, w_gate):
+def sizes(latent_keys, rope_keys, w_uv, moe_tokens, expert_ids, w_gate):
     heads, latent, value = w_uv.shape
     tokens, width = moe_tokens.shape
     return dict(
@@ -927,6 +1005,7 @@
         turn=rope_keys.shape[0],
         value=value,
         tokens=tokens,
+        top=expert_ids.shape[1],
     )
 
 
@@ -945,29 +1024,35 @@
 def fused(n, attention_in, moe_in):
     moe_tokens, norm_gain, expert_ids, route_scale, w_gate, w_up, w_down = moe_in
     anywhere = pl.BlockSpec(memory_space=pl.ANY)
-    whole = pl.BlockSpec(memory_space=pltpu.VMEM)
     total = n["width"] * lax.axis_size("ctx")
     attn_shape = jax.ShapeDtypeStruct((n["seq"], n["heads"] * n["value"]), bf16)
     rows_shape = jax.ShapeDtypeStruct((n["tokens"], n["width"]), bf16)
+    last_shape = jax.ShapeDtypeStruct((n["rows"], n["width"]), bf16)
     parts = pl.pallas_call(
         functools.partial(expert_kernel, n["nz"], CHUNKS, total),
-        out_shape=(attn_shape, rows_shape, rows_shape, rows_shape),
-        in_specs=[anywhere] * 9 + [whole] * 3,
+        out_shape=(attn_shape, rows_shape, last_shape, last_shape),
+        in_specs=[anywhere] * 12,
         out_specs=(anywhere,) * 4,
         scratch_shapes=expert_scratch(**n),
         compiler_params=pltpu.CompilerParams(
             collective_id=0, has_side_effects=True, vmem_limit_bytes=VMEM_BYTES
         ),
     )(*attention_in, moe_tokens, w_gate, w_up, w_down, norm_gain, expert_ids.T, route_scale.T)
-    steps = STEPS if n["seq"] % (16 * STEPS) == 0 and n["tokens"] % (16 * STEPS) == 0 else 1
-    attn_block = pl.BlockSpec((n["seq"] // steps, attn_shape.shape[1]), lambda i: (i, 0))
-    rows_block = pl.BlockSpec((n["tokens"] // steps, n["width"]), lambda i: (i, 0))
+    dma = pltpu.SemaphoreType.DMA
     return pl.pallas_call(
-        functools.partial(gather_kernel, n["nz"] - 1),
-        grid=(steps,),
+        functools.partial(gather_kernel, n["nz"] - 1, CHUNKS),
         out_shape=(attn_shape, rows_shape),
-        in_specs=[attn_block] + [rows_block] * 3,
-        out_specs=(attn_block, rows_block),
+        in_specs=[anywhere] * 4,
+        out_specs=(anywhere, anywhere),
+        scratch_shapes=[
+            pltpu.VMEM(attn_shape.shape, bf16),
+            pltpu.VMEM((CHUNKS, n["rows"], n["width"]), bf16),
+            pltpu.VMEM(last_shape.shape, bf16),
+            pltpu.VMEM(last_shape.shape, bf16),
+            dma((CHUNKS + 3,)),
+            dma((CHUNKS + 1,)),
+        ],
+        compiler_params=pltpu.CompilerParams(vmem_limit_bytes=VMEM_BYTES),
     )(*parts)
 
 
@@ -985,7 +1070,7 @@
     w_up,
     w_down,
 ):
-    n = sizes(latent_keys, rope_keys, w_uv, moe_tokens, w_gate)
+    n = sizes(latent_keys, rope_keys, w_uv, moe_tokens, expert_ids, w_gate)
     if not fits(n, w_gate):
         return hop_body(
             q_latent,

time: 170 us -> 168 us (0.988)
  Pallas kernels: 169 us -> 167 us
where the time goes in v3:
time: 168 us
  Pallas kernels  167 us (99%)
    pallas_call x1, Pallas kernels, fused(): pl.pallas_call(functools.partial(expert_kernel, n['nz'], CHUNKS, total),...  164 us

profile of v3, /device:TPU:0, one launch (start us, length us, event | category | flops | bytes accessed | tf_op | source)
XLA Modules:
  0.0 168.0 jit_solution(29599923033436662)
XLA Ops:
  0.6 164.4 %shard_map.131 = (bf16[128,512]{1,0:T(8,128)(2,1)}, bf16[256,3584]{1,0:T(8,128)(2,1)}, bf16[64,3584]{1,0:T(8,128)(2,1)}, bf16[64,3584]{1,0:T(8,128)(2,1)}) custom-call(bf16[128,2048]{1,0:T(8,128)(2,1)} %ql_hbm.1, bf16[128,256]{1,0:T(8,128)(2,1)} %qr_hbm.1, bf16[512,128]{1,0:T(8,128)(2,1)} %lk_hbm.1, bf16[64,128]{1,0:T(8,128)(2,1)} %rk_hbm.1, ...), custom_call_target="tpu_custom_call" | custom-call | tf_op jit(solution)/shard_map/pallas_call | solution.py:1031
  165.0 2.9 %shard_map.132 = (bf16[128,512]{1,0:T(8,128)(2,1)}, bf16[256,3584]{1,0:T(8,128)(2,1)}) custom-call(bf16[128,512]{1,0:T(8,128)(2,1)} %get-tuple-element.6.attn_in, bf16[256,3584]{1,0:T(8,128)(2,1)} %get-tuple-element.7.own_in, bf16[64,3584]{1,0:T(8,128)(2,1)} %get-tuple-element.8.right_in, bf16[64,3584]{1,0:T(8,128)(2,1)} %get-tuple-element.9.left_in), custom_call_target="tpu_custom_call" | custom-call | tf_op jit(solution)/shard_map/pallas_call | solution.py:1042

commit v4 on v3

--- a/solution.py
+++ b/solution.py
@@ -489,9 +489,6 @@
             (update / whole).astype(bf16), uv[head]
         ).astype(bf16)
 
-    for i in range(chunks):
-        own_rows(i).start()
-
     small = [
         pltpu.make_async_copy(src, dst, s_sem.at[n])
         for n, (src, dst) in enumerate(
@@ -500,6 +497,32 @@
     ]
     for copy in small:
         copy.start()
+    for i in range(chunks):
+        own_rows(i).start()
+
+    @pl.when((z == 0) | (z == last))
+    def _():
+        pl.semaphore_wait(barrier, 3)
+
+    @pl.when((z > 0) & (z < last))
+    def _():
+        pl.semaphore_wait(barrier, 4)
+
+    for i in range(half):
+        own_rows(i).wait()
+
+        @pl.when(z < last)
+        def _():
+            give_rows(i, True).start()
+
+        @pl.when(z > 0)
+        def _():
+            give_rows(i, False).start()
+
+    def give_rest(to_right):
+        for i in range(half, chunks):
+            give_rows(i, to_right).start()
+
     ropes[0, turn:, :] = jnp.zeros((turn, ropes.shape[2]), bf16)
     ropes[1, :turn, :] = jnp.zeros((turn, ropes.shape[2]), bf16)
     for copy in small:
@@ -512,14 +535,6 @@
             )
         routes[z, expert] = line
 
-    @pl.when((z == 0) | (z == last))
-    def _():
-        pl.semaphore_wait(barrier, 3)
-
-    @pl.when((z > 0) & (z < last))
-    def _():
-        pl.semaphore_wait(barrier, 4)
-
     @pl.when(z < last)
     def _():
         pass_routes(z, True).start()
@@ -527,21 +542,6 @@
     @pl.when(z > 0)
     def _():
         pass_routes(z, False).start()
-
-    for i in range(half):
-        own_rows(i).wait()
-
-        @pl.when(z < last)
-        def _():
-            give_rows(i, True).start()
-
-        @pl.when(z > 0)
-        def _():
-            give_rows(i, False).start()
-
-    def give_rest(to_right):
-        for i in range(half, chunks):
-            give_rows(i, to_right).start()
 
     for k in range(2):
         own_weights(k).start()
@@ -740,7 +740,7 @@
                 def _():
                     pass_rows(at, to_right).start()
 
-                @pl.when(i == 0)
+                @pl.when(i == half - 1)
                 def _():
                     pass_routes(source, to_right).wait_recv()
 
@@ -854,7 +854,7 @@
                 def _():
                     pass_rows(source * chunks + i, to_right).wait_send()
 
-                @pl.when(onward & (i == 0))
+                @pl.when(onward & (i == half - 1))
                 def _():
                     pass_routes(source, to_right).wait_send()
 

time: 168 us -> 168 us (level)
  no operation moved by 1% of the time
where the time goes in v4:
time: 168 us
  Pallas kernels  167 us (99%)
    pallas_call x1, Pallas kernels, fused(): pl.pallas_call(functools.partial(expert_kernel, n['nz'], CHUNKS, total),...  164 us

profile of v4, /device:TPU:0, one launch (start us, length us, event | category | flops | bytes accessed | tf_op | source)
XLA Modules:
  0.0 167.9 jit_solution(12082827199426768534)
XLA Ops:
  0.6 164.3 %shard_map.131 = (bf16[128,512]{1,0:T(8,128)(2,1)}, bf16[256,3584]{1,0:T(8,128)(2,1)}, bf16[64,3584]{1,0:T(8,128)(2,1)}, bf16[64,3584]{1,0:T(8,128)(2,1)}) custom-call(bf16[128,2048]{1,0:T(8,128)(2,1)} %ql_hbm.1, bf16[128,256]{1,0:T(8,128)(2,1)} %qr_hbm.1, bf16[512,128]{1,0:T(8,128)(2,1)} %lk_hbm.1, bf16[64,128]{1,0:T(8,128)(2,1)} %rk_hbm.1, ...), custom_call_target="tpu_custom_call" | custom-call | tf_op jit(solution)/shard_map/pallas_call | solution.py:1031
  165.0 2.9 %shard_map.132 = (bf16[128,512]{1,0:T(8,128)(2,1)}, bf16[256,3584]{1,0:T(8,128)(2,1)}) custom-call(bf16[128,512]{1,0:T(8,128)(2,1)} %get-tuple-element.6.attn_in, bf16[256,3584]{1,0:T(8,128)(2,1)} %get-tuple-element.7.own_in, bf16[64,3584]{1,0:T(8,128)(2,1)} %get-tuple-element.8.right_in, bf16[64,3584]{1,0:T(8,128)(2,1)} %get-tuple-element.9.left_in), custom_call_target="tpu_custom_call" | custom-call | tf_op jit(solution)/shard_map/pallas_call | solution.py:1042
